TPU v7x, 32 devices: a whole 2x2x4 slice. The times are simulated.
32 devices in a mesh: fsdp: 8 (over z, x), rep: 4 (over y, core).
Axes of the slice: x: 2, y: 2, z: 4, core: 2. Of those that a mesh axis runs over, the one named last changes fastest.
Arguments:
- partials: bfloat16 [4, 56, 1024, 1024], P('rep', None, 'fsdp'), may hold values from -400 to 400
- sketch: bfloat16 [8, 4, 2, 1024, 256], P('fsdp', 'rep'), may hold values from -3 to 3
- owner_table: int32 [56, 1], replicated, may hold values from 0 to 7; in each aligned block of 14 rows (0 to 13, 14 to 27, ...) at most 2 rows name the same one
Outputs:
- update: bfloat16 [56, 1024, 1024], P('rep', 'fsdp')
- new_sketch: bfloat16 [8, 4, 2, 1024, 256], P('fsdp', 'rep')
Inputs may be any that keep to these rules, and one draw needn't show every extreme that they name: `owner_table`: in each aligned slice of 14 blocks no owner holds more than 2 blocks; some owner holds exactly 2 in some slice.
All inputs are finite; a program needn't handle non-finite values.
Results may differ from a plain program's by a relative error of at most 0.015.
Values may be sent and summed in bfloat16 or wider, within the bound.
A program may use at most 128 MiB of HBM per device.

v0:
```python
import functools
import math

import jax
import jax.numpy as jnp
from jax import lax
from jax.experimental import pallas as pl
from jax.experimental.pallas import tpu as pltpu
from jax.sharding import PartitionSpec as P

NS_ITERS = 5


DECAY = 0.9
DAMPING = 64.0
FIRST_AXES = (((0,), (0,)), ((), ()))
LAST_AXES = (((1,), (1,)), ((), ()))


def inverse_root(matrix, epsilon):
    identity = jnp.eye(matrix.shape[0], dtype=jnp.float32)
    trace_sum = jnp.trace(matrix) + epsilon
    current = matrix / trace_sum
    inverse = identity
    for repeat in range(NS_ITERS):
        middle = 1.5 * identity - 0.5 * jnp.dot(inverse, current, precision=lax.Precision.HIGHEST)
        current = jnp.dot(current, middle, precision=lax.Precision.HIGHEST)
        inverse = jnp.dot(middle, inverse, precision=lax.Precision.HIGHEST)
    return inverse / jnp.sqrt(trace_sum)


def precondition(gradient, current_sketch):
    identity = jnp.eye(current_sketch.shape[1], dtype=jnp.float32)
    projected = lax.dot_general(
        gradient, current_sketch, FIRST_AXES, preferred_element_type=jnp.float32
    ).astype(jnp.bfloat16)
    gram_matrix = lax.dot_general(
        current_sketch, current_sketch, FIRST_AXES, preferred_element_type=jnp.float32
    ).astype(jnp.bfloat16)
    powered = DECAY * jnp.dot(
        current_sketch, gram_matrix, preferred_element_type=jnp.float32
    ) + jnp.dot(gradient, projected, preferred_element_type=jnp.float32)
    inner_gram = lax.dot_general(powered, powered, FIRST_AXES, precision=lax.Precision.HIGHEST)
    basis_full = jnp.dot(powered, inverse_root(inner_gram, 1e-06), precision=lax.Precision.HIGHEST)
    basis_low = basis_full.astype(jnp.bfloat16)
    coefficients = lax.dot_general(
        gradient, basis_low, FIRST_AXES, preferred_element_type=jnp.float32
    ).astype(jnp.bfloat16)
    alignment = lax.dot_general(
        current_sketch, basis_low, FIRST_AXES, preferred_element_type=jnp.float32
    )
    energy = DECAY * lax.dot_general(
        alignment, alignment, FIRST_AXES, precision=lax.Precision.HIGHEST
    ) + lax.dot_general(coefficients, coefficients, FIRST_AXES, preferred_element_type=jnp.float32)
    root_inverse = inverse_root(energy + DAMPING * identity, 0.0)
    inner_part = jnp.dot(energy, root_inverse, precision=lax.Precision.HIGHEST)
    new_block = jnp.dot(basis_full, inner_part, precision=lax.Precision.HIGHEST).astype(
        jnp.bfloat16
    )
    mix_matrix = math.sqrt(DAMPING) * root_inverse - identity
    side_terms = lax.dot_general(
        coefficients.astype(jnp.float32), mix_matrix, LAST_AXES, precision=lax.Precision.HIGHEST
    ).astype(jnp.bfloat16)
    update_block = (
        gradient.astype(jnp.float32)
        + lax.dot_general(basis_low, side_terms, LAST_AXES, preferred_element_type=jnp.float32)
    ).astype(jnp.bfloat16)
    return (update_block, new_block)


def squared_sum(values):
    wide = values.astype(jnp.float32)
    return jnp.sum(wide * wide)


def process_slot(slot_index, arrived, clip_factor, held_sketches, filled):
    block_width = arrived.shape[-1]
    gradient = (clip_factor * arrived.reshape(block_width, block_width).astype(jnp.float32)).astype(
        jnp.bfloat16
    )
    current_sketch = held_sketches[slot_index]
    active = slot_index < filled
    update_block, new_block = precondition(gradient, current_sketch)
    new_block = jnp.where(active, new_block, current_sketch)
    return (update_block, new_block)


def local(partials, sketch, owner_table):
    block_total = partials.shape[1]
    row_count = partials.shape[2]
    block_width = partials.shape[3]
    fsdp_count = lax.axis_size("fsdp")
    per_slice = block_total // lax.axis_size("rep")
    slot_count = sketch.shape[2]
    reduced = lax.psum_scatter(
        partials[0].astype(jnp.float32).astype(jnp.bfloat16), "rep", scatter_dimension=0, tiled=True
    )
    my_owners = lax.dynamic_slice_in_dim(
        owner_table[:, 0], lax.axis_index("rep") * per_slice, per_slice
    )
    positions = jnp.arange(per_slice, dtype=jnp.int32)
    same_owner = (my_owners[:, None] == my_owners[None, :]) & (
        positions[:, None] < positions[None, :]
    )
    rank_in = jnp.sum(same_owner.astype(jnp.int32), axis=0)
    target = rank_in * fsdp_count + my_owners
    selector = (
        target[None, :] == jnp.arange(slot_count * fsdp_count, dtype=jnp.int32)[:, None]
    ).astype(jnp.bfloat16)
    flattened = reduced.reshape(per_slice, row_count * block_width)
    outgoing = jnp.dot(selector, flattened, preferred_element_type=jnp.float32).astype(jnp.bfloat16)
    outgoing = outgoing.reshape(slot_count, fsdp_count, row_count, block_width)
    sum_squares = lax.psum(squared_sum(reduced), ("fsdp", "rep"))
    clip_limit = 0.5 * math.sqrt(block_total * block_width * block_width)
    clip_factor = jnp.minimum(1.0, clip_limit / jnp.sqrt(sum_squares + 1e-06))
    filled = jnp.sum((my_owners == lax.axis_index("fsdp")).astype(jnp.int32))
    held_sketches = sketch[0, 0]
    fresh_list = []
    incoming = lax.all_to_all(outgoing, "fsdp", split_axis=1, concat_axis=1, tiled=True)
    update_list = []
    for slot_index in range(slot_count):
        update_block, new_block = process_slot(
            slot_index, incoming[slot_index], clip_factor, held_sketches, filled
        )
        update_list.append(update_block)
        fresh_list.append(new_block)
    stacked = jnp.stack(update_list).reshape(slot_count, fsdp_count, row_count, block_width)
    returned = lax.all_to_all(stacked, "fsdp", split_axis=1, concat_axis=1, tiled=True)
    returned = returned.reshape(slot_count * fsdp_count, row_count * block_width)
    my_updates = lax.dot_general(
        selector, returned, FIRST_AXES, preferred_element_type=jnp.float32
    ).astype(jnp.bfloat16)
    my_updates = my_updates.reshape(per_slice, row_count, block_width)
    return (my_updates, jnp.stack(fresh_list)[None, None])

MESH = pl.DeviceIdType.MESH
BF = jnp.bfloat16
F32 = jnp.float32


def flip(value, mask, bits):
    result = 0
    for bit in range(bits):
        ours = (value // (1 << bit)) % 2
        theirs = (mask // (1 << bit)) % 2
        result = result + (ours + theirs - 2 * ours * theirs) * (1 << bit)
    return result


def greet(peers):
    barrier = pltpu.get_barrier_semaphore()
    for peer in peers:
        pl.semaphore_signal(barrier, inc=1, device_id=peer, device_id_type=MESH)
    pl.semaphore_wait(barrier, len(peers))


def remote(source, target, send_sem, recv_sem, peer):
    return pltpu.make_async_remote_copy(
        src_ref=source,
        dst_ref=target,
        send_sem=send_sem,
        recv_sem=recv_sem,
        device_id=peer,
        device_id_type=MESH,
    )


def mm(a, b):
    return jnp.dot(a, b, preferred_element_type=F32)


def mm_last(a, b):
    return lax.dot_general(a, b, LAST_AXES, preferred_element_type=F32)


def split(values):
    high = values.astype(BF)
    return high, (values - high.astype(F32)).astype(BF)


def mm3(a, b):
    return mm(a[0], b[0]) + (mm(a[0], b[1]) + mm(a[1], b[0]))


def eye_of(size):
    return (
        lax.broadcasted_iota(jnp.int32, (size, size), 0)
        == lax.broadcasted_iota(jnp.int32, (size, size), 1)
    ).astype(F32)


def kernel_root(matrix, epsilon, identity):
    trace_sum = jnp.sum(matrix * identity, keepdims=True) + epsilon
    current = matrix / trace_sum
    middle = 1.5 * identity - 0.5 * current
    middle_s = split(middle)
    inverse_s = middle_s
    current_s = split(mm3(split(current), middle_s))
    for repeat in range(1, NS_ITERS):
        middle_s = split(1.5 * identity - 0.5 * mm3(inverse_s, current_s))
        if repeat < NS_ITERS - 1:
            current_s = split(mm3(current_s, middle_s))
        inverse = mm3(middle_s, inverse_s)
        inverse_s = split(inverse)
    return inverse / jnp.sqrt(trace_sum)


def step_kernel(
    fsdp, slots, per_slice, clip_limit, owners_ref, sketch_ref, partials_ref, returned_ref, fresh_ref,
    held_far, held_own, paired_far, paired_own, far, crossed, summed, incoming, updates, narrow_t, side_t, wide, basis, basis_low,
    square_acc, rep_squares, fsdp_squares, table, scalars,
    load_sems, pair_sems, cross_sems, owner_sems, rep_sems, fsdp_sems, home_sems, self_sems, table_sem,
):
    bits = fsdp.bit_length() - 1
    half = fsdp // 2
    steps = slots * fsdp
    rows = incoming.shape[2]
    width = incoming.shape[3]
    rank = sketch_ref.shape[2]
    tile = rank
    me_f = lax.axis_index("fsdp")
    me_r = lax.axis_index("rep")
    core = me_r % 2
    row = me_r // 2
    partner = row * 2 + 1 - core
    across = (1 - row) * 2 + core
    partner_across = (1 - row) * 2 + 1 - core

    def blocks_of(number):
        return partials_ref.at[0, pl.ds(number * per_slice, per_slice)]

    loads = [
        pltpu.make_async_copy(blocks_of(across), held_far, load_sems.at[0]),
        pltpu.make_async_copy(blocks_of(me_r), held_own, load_sems.at[1]),
    ]
    pairs = [
        remote(
            blocks_of(theirs), landing, pair_sems.at[0, n], pair_sems.at[1, n], {"rep": partner}
        )
        for n, (theirs, landing) in enumerate(
            ((partner_across, paired_far), (partner, paired_own))
        )
    ]
    loads[0].start()
    fill_table(fsdp, slots, per_slice, owners_ref, table)
    greet(
        [{"rep": (me_r + d) % 4} for d in range(1, 4)]
        + [{"fsdp": (me_f + d) % fsdp} for d in range(1, fsdp)]
    )
    pairs[0].start()
    pairs[1].start()
    loads[1].start()
    publish = pltpu.make_async_copy(table, scalars, table_sem)
    publish.start()
    square_acc[...] = jnp.zeros_like(square_acc)
    publish.wait()
    loads[0].wait()
    pairs[0].wait_recv()

    def where(i):
        group = i // (slots * half)
        slot = (i % (slots * half)) // half
        mask = fsdp - 1 - half * group - i % half
        return slot, mask, flip(me_f, mask, bits)

    def cross_copy(i):
        return remote(
            far.at[i], crossed.at[i], cross_sems.at[0, i], cross_sems.at[1, i], {"rep": across}
        )

    def owner_copy(i):
        slot, mask, owner = where(i)
        return remote(
            summed.at[i],
            incoming.at[slot, me_f],
            owner_sems.at[0, i],
            owner_sems.at[1, i],
            {"fsdp": owner},
        )

    def send_across(i):
        slot, mask, owner = where(i)
        number = scalars[0, across * steps + slot * fsdp + owner]
        far[i] = (held_far[number].astype(F32) + paired_far[number].astype(F32)).astype(BF)
        cross_copy(i).start()

    def send_owner(i):
        slot, mask, owner = where(i)
        place = me_r * steps + slot * fsdp + owner
        number = scalars[0, place]
        cross_copy(i).wait_recv()
        pair = held_own[number].astype(F32) + paired_own[number].astype(F32)
        total = (pair + crossed[i].astype(F32)).astype(BF)

        @pl.when(mask == 0)
        def _():
            incoming[slot, me_f] = total

        @pl.when(mask != 0)
        def _():
            summed[i] = total
            owner_copy(i).start()

        wide_total = total.astype(F32)
        folded = jnp.sum((wide_total * wide_total).reshape(rows // 8, 8, width), axis=0)
        square_acc[...] += jnp.where(scalars[1, place] > 0, folded, 0.0)

    lag = 2

    def first(i, carry):
        send_across(i)
        return carry

    lax.fori_loop(0, lag, first, 0)
    loads[1].wait()
    pairs[1].wait_recv()

    def both(i, carry):
        @pl.when(i < steps - lag)
        def _():
            send_across(i + lag)

        send_owner(i)
        return carry

    lax.fori_loop(0, steps, both, 0)

    def arrived(k):
        def wait_one(n, carry):
            i = (n // half) * (slots * half) + k * half + n % half
            owner_copy(i).wait_recv()
            return carry

        lax.fori_loop(0, fsdp - 1, wait_one, 0)

    def wide_part(k, part):
        return incoming[k, :, :, part * tile : (part + 1) * tile].reshape(width, tile)

    def project(k, left_t, factor):
        for part in range(width // tile):
            product = mm(left_t, wide_part(k, part))
            if factor is not None:
                product = factor * product
            narrow_t[:, part * tile : (part + 1) * tile] = product.astype(BF)

    lanes = square_acc[:, 0:128]
    for part in range(1, width // 128):
        lanes = lanes + square_acc[:, part * 128 : (part + 1) * 128]
    rep_squares[me_r] = lanes
    rep_copies = [
        remote(
            rep_squares.at[me_r], rep_squares.at[me_r], rep_sems.at[0, d], rep_sems.at[1, d],
            {"rep": (me_r + d) % 4},
        )
        for d in range(1, 4)
    ]
    for copy in rep_copies:
        copy.start()
    arrived(0)
    sketch_t = sketch_ref[0].T
    project(0, sketch_t, None)
    for copy in rep_copies:
        copy.wait()
    lanes = rep_squares[0]
    for r in range(1, 4):
        lanes = lanes + rep_squares[r]
    fsdp_squares[me_f] = lanes
    fsdp_copies = [
        remote(
            fsdp_squares.at[me_f], fsdp_squares.at[me_f], fsdp_sems.at[0, d], fsdp_sems.at[1, d],
            {"fsdp": (me_f + d) % fsdp},
        )
        for d in range(1, fsdp)
    ]
    for copy in fsdp_copies:
        copy.start()
    identity = eye_of(rank)

    def home_copy(k, i):
        home = flip(me_f, fsdp - 1 - i, bits)
        return remote(
            updates.at[k, i], returned_ref.at[k, me_f], home_sems.at[0, k, i], home_sems.at[1, k, i],
            {"fsdp": home},
        )

    def self_copy(k):
        return pltpu.make_async_copy(
            updates.at[k, fsdp - 1], returned_ref.at[k, me_f], self_sems.at[k]
        )

    clip_factor = None
    for k in range(slots):
        sketch = sketch_ref[k]
        if k > 0:
            arrived(k)
            sketch_t = sketch.T
            project(k, sketch_t, None)
        gram = mm(sketch_t, sketch).astype(BF)
        projected_t = narrow_t[...]
        for part in range(fsdp):
            span = slice(part * rows, (part + 1) * rows)
            wide[span] = mm_last(incoming[k, part], projected_t)
            basis[span] = DECAY * mm(sketch[span], gram)
        if k == 0:
            for copy in fsdp_copies:
                copy.wait()
            lanes = fsdp_squares[0]
            for f in range(1, fsdp):
                lanes = lanes + fsdp_squares[f]
            sum_squares = jnp.sum(lanes, keepdims=True)
            clip_factor = jnp.minimum(1.0, clip_limit / jnp.sqrt(sum_squares + 1e-06))
        powered_s = split(basis[...] + (clip_factor * clip_factor) * wide[...])
        powered_t = powered_s[0].T
        mixed = mm(powered_t, powered_s[1])
        inner = mm(powered_t, powered_s[0]) + (mixed + mixed.T)
        root = split(kernel_root(inner, 1e-06, identity))
        full = mm3(powered_s, root)
        basis[...] = full
        low = full.astype(BF)
        basis_low[...] = low
        project(k, low.T, clip_factor)
        coefficients_t = narrow_t[...]
        align_s = split(mm(sketch_t, low))
        align_t = (align_s[0].T, align_s[1].T)
        energy = DECAY * mm3(align_t, align_s) + mm_last(coefficients_t, coefficients_t)
        root_inverse = kernel_root(energy + DAMPING * identity, 0.0, identity)
        mix = split(math.sqrt(DAMPING) * root_inverse - identity)
        side_t[...] = (mm(mix[0], coefficients_t) + mm(mix[1], coefficients_t)).astype(BF)

        def send(i, carry):
            home = flip(me_f, fsdp - 1 - i, bits)
            start = pl.multiple_of(home * rows, rows)
            gradient = (clip_factor * incoming[k, home].astype(F32)).astype(BF).astype(F32)
            updates[k, i] = (
                gradient + mm(basis_low[pl.ds(start, rows), :], side_t[...])
            ).astype(BF)

            @pl.when(i == fsdp - 1)
            def _():
                self_copy(k).start()

            @pl.when(i != fsdp - 1)
            def _():
                home_copy(k, i).start()

            return carry

        lax.fori_loop(0, fsdp, send, 0)
        inner_part = split(mm3(split(energy), split(root_inverse)))
        new_block = mm3(split(basis[...]), inner_part).astype(BF)
        active = scalars[1, me_r * steps + k * fsdp + me_f]
        fresh_ref[k] = jnp.where(active > 0, new_block, sketch)

    pairs[0].wait_send()
    pairs[1].wait_send()

    def finish(i, carry):
        slot, mask, owner = where(i)
        cross_copy(i).wait_send()

        @pl.when(mask != 0)
        def _():
            owner_copy(i).wait_send()

        return carry

    lax.fori_loop(0, steps, finish, 0)

    def finish_home(i, carry):
        for k in range(slots):
            home_copy(k, i).wait()
        return carry

    lax.fori_loop(0, fsdp - 1, finish_home, 0)
    for k in range(slots):
        self_copy(k).wait()


def fill_table(fsdp, slots, per_slice, owners_ref, table):
    total = owners_ref.shape[0]
    steps = slots * fsdp
    shape = (total, total)
    down = lax.broadcasted_iota(jnp.int32, shape, 0)
    along = lax.broadcasted_iota(jnp.int32, shape, 1)
    owners = jnp.broadcast_to(owners_ref[...], shape)
    owners_along = jnp.sum(jnp.where(down == along, owners, 0), axis=0, keepdims=True)
    slice_down = down // per_slice
    slice_along = along // per_slice
    same = (owners == owners_along) & (slice_down == slice_along) & (along < down)
    ranks = jnp.sum(jnp.where(same, 1, 0), axis=1, keepdims=True)
    shape = (total, table.shape[1])
    block = lax.broadcasted_iota(jnp.int32, shape, 0)
    owned = jnp.broadcast_to(owners_ref[...], shape)
    target = (block // per_slice) * steps + jnp.broadcast_to(ranks, shape) * fsdp + owned
    hit = target == lax.broadcasted_iota(jnp.int32, shape, 1)
    number = jnp.sum(jnp.where(hit, block % per_slice, 0), axis=0, keepdims=True)
    table[0:1, :] = jnp.minimum(number, per_slice - 1)
    table[1:2, :] = jnp.sum(jnp.where(hit, 1, 0), axis=0, keepdims=True)


def place_kernel(fsdp, per_slice, owners_ref, returned_ref, update_ref, held, counts, in_sems, out_sems):
    base = lax.axis_index("rep") * per_slice
    last = returned_ref.shape[0] - 1
    for owner in range(fsdp):
        counts[owner] = 0
    takes, puts = [], []
    for b in range(per_slice):
        owner = owners_ref[base + b, 0]
        count = counts[owner]
        counts[owner] = count + 1
        takes.append(
            pltpu.make_async_copy(returned_ref.at[jnp.minimum(count, last), owner], held.at[b], in_sems.at[b])
        )
        takes[-1].start()
    for b in range(per_slice):
        takes[b].wait()
        puts.append(pltpu.make_async_copy(held.at[b], update_ref.at[b], out_sems.at[b]))
        puts[-1].start()
    for put in puts:
        put.wait()


def fused(partials, sketch, owner_table):
    block_total, rows, width = partials.shape[1:]
    rank = sketch.shape[4]
    fsdp = lax.axis_size("fsdp")
    rep = lax.axis_size("rep")
    slots = sketch.shape[2]
    per_slice = block_total // rep
    steps = slots * fsdp
    table_width = -(-rep * steps // 128) * 128
    hbm = pl.BlockSpec(memory_space=pl.ANY)
    vmem = pl.BlockSpec(memory_space=pltpu.VMEM)
    smem = pl.BlockSpec(memory_space=pltpu.SMEM)
    dma = pltpu.SemaphoreType.DMA
    block = (rows, width)
    clip_limit = 0.5 * math.sqrt(block_total * width * width)
    returned, fresh = pl.pallas_call(
        functools.partial(step_kernel, fsdp, slots, per_slice, clip_limit),
        out_shape=(
            jax.ShapeDtypeStruct((slots, fsdp) + block, BF),
            jax.ShapeDtypeStruct((slots, width, rank), BF),
        ),
        in_specs=[vmem, vmem, hbm],
        out_specs=(hbm, vmem),
        scratch_shapes=[
            pltpu.VMEM((per_slice,) + block, BF),
            pltpu.VMEM((per_slice,) + block, BF),
            pltpu.VMEM((per_slice,) + block, BF),
            pltpu.VMEM((per_slice,) + block, BF),
            pltpu.VMEM((steps,) + block, BF),
            pltpu.VMEM((steps,) + block, BF),
            pltpu.VMEM((steps,) + block, BF),
            pltpu.VMEM((slots, fsdp) + block, BF),
            pltpu.VMEM((slots, fsdp) + block, BF),
            pltpu.VMEM((rank, width), BF),
            pltpu.VMEM((rank, width), BF),
            pltpu.VMEM((width, rank), F32),
            pltpu.VMEM((width, rank), F32),
            pltpu.VMEM((width, rank), BF),
            pltpu.VMEM((8, width), F32),
            pltpu.VMEM((rep, 8, 128), F32),
            pltpu.VMEM((fsdp, 8, 128), F32),
            pltpu.VMEM((2, table_width), jnp.int32),
            pltpu.SMEM((2, table_width), jnp.int32),
            dma((2,)),
            dma((2, 2)),
            dma((2, steps)),
            dma((2, steps)),
            dma((2, rep)),
            dma((2, fsdp)),
            dma((2, slots, fsdp)),
            dma((slots,)),
            dma,
        ],
        compiler_params=pltpu.CompilerParams(
            collective_id=0, has_side_effects=True, vmem_limit_bytes=VMEM_BYTES
        ),
        name="step",
    )(owner_table, sketch[0, 0], partials)
    updates = pl.pallas_call(
        functools.partial(place_kernel, fsdp, per_slice),
        out_shape=jax.ShapeDtypeStruct((per_slice,) + block, BF),
        in_specs=[smem, hbm],
        out_specs=hbm,
        scratch_shapes=[
            pltpu.VMEM((per_slice,) + block, BF),
            pltpu.SMEM((fsdp,), jnp.int32),
            dma((per_slice,)),
            dma((per_slice,)),
        ],
        name="place",
    )(owner_table, returned)
    return (updates, fresh[None, None])


VMEM_BYTES = 60 * 1024 * 1024


def choose(partials, sketch, owner_table):
    block_total, rows, width = partials.shape[1:]
    fsdp = lax.axis_size("fsdp")
    rep = lax.axis_size("rep")
    steps = sketch.shape[2] * fsdp
    per_slice = block_total // rep
    pairs = rep == 4 and fsdp & (fsdp - 1) == 0
    needed = (4 * per_slice + 5 * steps) * rows * width * 2
    if pairs and needed < VMEM_BYTES - (12 << 20):
        return fused(partials, sketch, owner_table)
    return local(partials, sketch, owner_table)


def solution(mesh):
    placed = (P("rep", None, "fsdp", None), P("fsdp", "rep", None, None, None), P())
    return jax.shard_map(
        choose,
        mesh=mesh,
        in_specs=placed,
        out_specs=(P("rep", "fsdp", None), P("fsdp", "rep", None, None, None)),
        check_vma=False,
    )
```

profile of v0, /device:TPU:0, one launch (start us, length us, event | category | flops | bytes accessed | tf_op | source)
XLA Modules:
  0.0 233.0 jit_solution(8005124944476447050)
XLA Ops:
  0.6 1.4 copy.6.owners_ref
  2.0 225.4 %step.1 = (bf16[2,8,128,1024]{3,2,1,0:T(8,128)(2,1)}, bf16[2,1024,256]{2,1,0:T(8,128)(2,1)}) custom-call(s32[56,1]{1,0:T(8,128)} %copy.6.owners_ref, bf16[2,1024,256]{2,1,0:T(8,128)(2,1)} %bitcast.2, bf16[1,56,128,1024]{3,2,1,0:T(8,128)(2,1)} %partials_ref.1), custom_call_target="tpu_custom_call" | custom-call | tf_op jit(solution)/shard_map/step/pallas_call | solution.py:538
  227.4 0.0 copy-start
  227.4 4.5 %place.1 = bf16[14,128,1024]{2,1,0:T(8,128)(2,1)} custom-call(s32[56,1]{1,0:T(8,128)} %copy.6.owners_ref, bf16[2,8,128,1024]{3,2,1,0:T(8,128)(2,1)} %get-tuple-element.4.returned_ref), custom_call_target="tpu_custom_call" | custom-call | tf_op jit(solution)/shard_map/place/pallas_call | solution.py:581
  232.0 0.0 copy-done
  232.0 1.0 copy.8
Async XLA Ops:
  227.4 4.6 %copy-start = (bf16[2,1024,256]{2,1,0:T(8,128)(2,1)S(1)}, bf16[2,1024,256]{2,1,0:T(8,128)(2,1)}, u32[]{:S(2)}) copy-start(bf16[2,1024,256]{2,1,0:T(8,128)(2,1)} %get-tuple-element.5) | copy-start | bytes 3145732
where the time goes:
time: 233 us
  Pallas kernels  230 us (99%)
  local copies, waits for them, and re-layouts  2.33 us (1%)
    pallas_call x1, Pallas kernels, fused(): pl.pallas_call(functools.partial(step_kernel, fsdp, slots, per_slice, cli...  225 us

commit v1 on v0

--- a/solution.py
+++ b/solution.py
@@ -207,13 +207,14 @@
 
 def step_kernel(
     fsdp, slots, per_slice, clip_limit, owners_ref, sketch_ref, partials_ref, returned_ref, fresh_ref,
-    held_far, held_own, paired_far, paired_own, far, crossed, summed, incoming, updates, narrow_t, side_t, wide, basis, basis_low,
+    held_0, held_1, held_2, held_3, sketch_held, staged, paired, crossed, totals, summed, incoming, updates, narrow_t, side_t, wide, basis, basis_low,
     square_acc, rep_squares, fsdp_squares, table, scalars,
     load_sems, pair_sems, cross_sems, owner_sems, rep_sems, fsdp_sems, home_sems, self_sems, table_sem,
 ):
     bits = fsdp.bit_length() - 1
     half = fsdp // 2
     steps = slots * fsdp
+    empty = steps - per_slice
     rows = incoming.shape[2]
     width = incoming.shape[3]
     rank = sketch_ref.shape[2]
@@ -225,47 +226,61 @@
     partner = row * 2 + 1 - core
     across = (1 - row) * 2 + core
     partner_across = (1 - row) * 2 + 1 - core
-
-    def blocks_of(number):
-        return partials_ref.at[0, pl.ds(number * per_slice, per_slice)]
-
+    slices = (partner_across, partner, across, me_r)
+    held = (held_0, held_1, held_2, held_3)
     loads = [
-        pltpu.make_async_copy(blocks_of(across), held_far, load_sems.at[0]),
-        pltpu.make_async_copy(blocks_of(me_r), held_own, load_sems.at[1]),
+        pltpu.make_async_copy(
+            partials_ref.at[0, pl.ds(number * per_slice, per_slice)], held[n], load_sems.at[n]
+        )
+        for n, number in enumerate(slices)
     ]
-    pairs = [
-        remote(
-            blocks_of(theirs), landing, pair_sems.at[0, n], pair_sems.at[1, n], {"rep": partner}
-        )
-        for n, (theirs, landing) in enumerate(
-            ((partner_across, paired_far), (partner, paired_own))
-        )
-    ]
-    loads[0].start()
-    fill_table(fsdp, slots, per_slice, owners_ref, table)
+    loads.append(pltpu.make_async_copy(sketch_ref, sketch_held, load_sems.at[len(slices)]))
+    for load in loads:
+        load.start()
+    fill_table(fsdp, slots, per_slice, me_f, owners_ref, table)
+    publish = pltpu.make_async_copy(table, scalars, table_sem)
+    publish.start()
     greet(
         [{"rep": (me_r + d) % 4} for d in range(1, 4)]
         + [{"fsdp": (me_f + d) % fsdp} for d in range(1, fsdp)]
     )
-    pairs[0].start()
-    pairs[1].start()
-    loads[1].start()
-    publish = pltpu.make_async_copy(table, scalars, table_sem)
-    publish.start()
     square_acc[...] = jnp.zeros_like(square_acc)
     publish.wait()
     loads[0].wait()
-    pairs[0].wait_recv()
+    loads[1].wait()
+
+    def block_at(n, k):
+        return held[n][scalars[0, slices[n] * per_slice + k]]
+
+    def stage_ref(n, k):
+        return updates.at[k // fsdp, k % fsdp] if n == 0 else staged.at[k]
+
+    def pair_copy(n, k):
+        return remote(
+            stage_ref(n, k), paired.at[n, k], pair_sems.at[0, n, k], pair_sems.at[1, n, k], {"rep": partner}
+        )
+
+    def stage(k, carry):
+        for n in range(2):
+            stage_ref(n, k)[...] = block_at(n, k)
+            pair_copy(n, k).start()
+        return carry
+
+    lax.fori_loop(0, per_slice, stage, 0)
+    for n in range(empty):
+        totals[n] = jnp.zeros_like(totals[n])
+        totals[empty + per_slice + n] = jnp.zeros_like(totals[n])
+    for load in loads[2:]:
+        load.wait()
 
     def where(i):
-        group = i // (slots * half)
-        slot = (i % (slots * half)) // half
-        mask = fsdp - 1 - half * group - i % half
-        return slot, mask, flip(me_f, mask, bits)
-
-    def cross_copy(i):
+        place = i % fsdp
+        mask = fsdp - 1 - place // 2 - half * (place % 2)
+        return i // fsdp, mask, flip(me_f, mask, bits)
+
+    def cross_copy(k):
         return remote(
-            far.at[i], crossed.at[i], cross_sems.at[0, i], cross_sems.at[1, i], {"rep": across}
+            paired.at[0, k], crossed.at[k], cross_sems.at[0, k], cross_sems.at[1, k], {"rep": across}
         )
 
     def owner_copy(i):
@@ -278,19 +293,26 @@
             {"fsdp": owner},
         )
 
-    def send_across(i):
-        slot, mask, owner = where(i)
-        number = scalars[0, across * steps + slot * fsdp + owner]
-        far[i] = (held_far[number].astype(F32) + paired_far[number].astype(F32)).astype(BF)
-        cross_copy(i).start()
+    def send_across(k):
+        pair_copy(0, k).wait_recv()
+        paired[0, k] = (block_at(2, k).astype(F32) + paired[0, k].astype(F32)).astype(BF)
+        cross_copy(k).start()
+
+    def add_up(k):
+        pair_copy(1, k).wait_recv()
+        pair = block_at(3, k).astype(F32) + paired[1, k].astype(F32)
+        cross_copy(k).wait_recv()
+        total = (pair + crossed[k].astype(F32)).astype(BF)
+        totals[empty + k] = total
+        wide_total = total.astype(F32)
+        square_acc[...] += jnp.sum((wide_total * wide_total).reshape(rows // 8, 8, width), axis=0)
 
     def send_owner(i):
         slot, mask, owner = where(i)
-        place = me_r * steps + slot * fsdp + owner
-        number = scalars[0, place]
-        cross_copy(i).wait_recv()
-        pair = held_own[number].astype(F32) + paired_own[number].astype(F32)
-        total = (pair + crossed[i].astype(F32)).astype(BF)
+        skipped = scalars[1, me_r * steps + i]
+        total = totals[empty + i]
+        for n in range(1, empty + 1):
+            total = jnp.where(skipped == n, totals[empty + i - n], total)
 
         @pl.when(mask == 0)
         def _():
@@ -301,34 +323,28 @@
             summed[i] = total
             owner_copy(i).start()
 
-        wide_total = total.astype(F32)
-        folded = jnp.sum((wide_total * wide_total).reshape(rows // 8, 8, width), axis=0)
-        square_acc[...] += jnp.where(scalars[1, place] > 0, folded, 0.0)
-
-    lag = 2
-
-    def first(i, carry):
-        send_across(i)
+    lag = 3
+
+    def first(k, carry):
+        send_across(k)
         return carry
 
     lax.fori_loop(0, lag, first, 0)
-    loads[1].wait()
-    pairs[1].wait_recv()
-
-    def both(i, carry):
-        @pl.when(i < steps - lag)
+
+    def both(k, carry):
+        @pl.when(k < per_slice - lag)
         def _():
-            send_across(i + lag)
-
-        send_owner(i)
+            send_across(k + lag)
+
+        add_up(k)
+        send_owner(k)
         return carry
 
-    lax.fori_loop(0, steps, both, 0)
+    lax.fori_loop(0, per_slice, both, 0)
 
     def arrived(k):
         def wait_one(n, carry):
-            i = (n // half) * (slots * half) + k * half + n % half
-            owner_copy(i).wait_recv()
+            owner_copy(k * fsdp + n).wait_recv()
             return carry
 
         lax.fori_loop(0, fsdp - 1, wait_one, 0)
@@ -357,7 +373,7 @@
     for copy in rep_copies:
         copy.start()
     arrived(0)
-    sketch_t = sketch_ref[0].T
+    sketch_t = sketch_held[0].T
     project(0, sketch_t, None)
     for copy in rep_copies:
         copy.wait()
@@ -374,10 +390,24 @@
     ]
     for copy in fsdp_copies:
         copy.start()
+
+    def last(i, carry):
+        send_owner(i)
+        return carry
+
+    lax.fori_loop(per_slice, steps, last, 0)
+
+    def staged_out(k, carry):
+        for n in range(2):
+            pair_copy(n, k).wait_send()
+        cross_copy(k).wait_send()
+        return carry
+
+    lax.fori_loop(0, per_slice, staged_out, 0)
     identity = eye_of(rank)
 
     def home_copy(k, i):
-        home = flip(me_f, fsdp - 1 - i, bits)
+        home = flip(me_f, fsdp - 1 - i // 2 - half * (i % 2), bits)
         return remote(
             updates.at[k, i], returned_ref.at[k, me_f], home_sems.at[0, k, i], home_sems.at[1, k, i],
             {"fsdp": home},
@@ -390,7 +420,7 @@
 
     clip_factor = None
     for k in range(slots):
-        sketch = sketch_ref[k]
+        sketch = sketch_held[k]
         if k > 0:
             arrived(k)
             sketch_t = sketch.T
@@ -428,7 +458,7 @@
         side_t[...] = (mm(mix[0], coefficients_t) + mm(mix[1], coefficients_t)).astype(BF)
 
         def send(i, carry):
-            home = flip(me_f, fsdp - 1 - i, bits)
+            home = flip(me_f, fsdp - 1 - i // 2 - half * (i % 2), bits)
             start = pl.multiple_of(home * rows, rows)
             gradient = (clip_factor * incoming[k, home].astype(F32)).astype(BF).astype(F32)
             updates[k, i] = (
@@ -448,15 +478,11 @@
         lax.fori_loop(0, fsdp, send, 0)
         inner_part = split(mm3(split(energy), split(root_inverse)))
         new_block = mm3(split(basis[...]), inner_part).astype(BF)
-        active = scalars[1, me_r * steps + k * fsdp + me_f]
+        active = scalars[2, me_r * steps + k * fsdp + fsdp - 1]
         fresh_ref[k] = jnp.where(active > 0, new_block, sketch)
-
-    pairs[0].wait_send()
-    pairs[1].wait_send()
 
     def finish(i, carry):
         slot, mask, owner = where(i)
-        cross_copy(i).wait_send()
 
         @pl.when(mask != 0)
         def _():
@@ -476,26 +502,40 @@
         self_copy(k).wait()
 
 
-def fill_table(fsdp, slots, per_slice, owners_ref, table):
-    total = owners_ref.shape[0]
+def fill_table(fsdp, slots, per_slice, me_f, owners_ref, table):
+    total = owners_ref.shape[1]
     steps = slots * fsdp
+    half = fsdp // 2
     shape = (total, total)
     down = lax.broadcasted_iota(jnp.int32, shape, 0)
     along = lax.broadcasted_iota(jnp.int32, shape, 1)
-    owners = jnp.broadcast_to(owners_ref[...], shape)
-    owners_along = jnp.sum(jnp.where(down == along, owners, 0), axis=0, keepdims=True)
-    slice_down = down // per_slice
-    slice_along = along // per_slice
-    same = (owners == owners_along) & (slice_down == slice_along) & (along < down)
-    ranks = jnp.sum(jnp.where(same, 1, 0), axis=1, keepdims=True)
+
+    def turned(values):
+        return jnp.sum(jnp.where(down == along, values, 0), axis=0, keepdims=True)
+
+    owners_along = jnp.broadcast_to(owners_ref[...], shape)
+    owners = jnp.sum(jnp.where(down == along, owners_along, 0), axis=1, keepdims=True)
+    owners = jnp.broadcast_to(owners, shape)
+    same = down // per_slice == along // per_slice
+    earlier = same & (owners == owners_along) & (along < down)
+    ranks = jnp.sum(jnp.where(earlier, 1, 0), axis=1, keepdims=True)
+    mask = lax.bitwise_xor(owners, jnp.full(shape, me_f, jnp.int32))
+    place = jnp.where(mask >= half, 2 * (fsdp - 1 - mask), 2 * (half - 1 - mask) + 1)
+    spot = jnp.broadcast_to(ranks, shape) * fsdp + place
+    ahead = jnp.sum(jnp.where(same & (turned(spot) < spot), 1, 0), axis=1, keepdims=True)
+    spots = jnp.max(spot, axis=1, keepdims=True)
     shape = (total, table.shape[1])
     block = lax.broadcasted_iota(jnp.int32, shape, 0)
-    owned = jnp.broadcast_to(owners_ref[...], shape)
-    target = (block // per_slice) * steps + jnp.broadcast_to(ranks, shape) * fsdp + owned
-    hit = target == lax.broadcasted_iota(jnp.int32, shape, 1)
+    lane = lax.broadcasted_iota(jnp.int32, shape, 1)
+    group = block // per_slice
+    hit = group * per_slice + jnp.broadcast_to(ahead, shape) == lane
     number = jnp.sum(jnp.where(hit, block % per_slice, 0), axis=0, keepdims=True)
     table[0:1, :] = jnp.minimum(number, per_slice - 1)
-    table[1:2, :] = jnp.sum(jnp.where(hit, 1, 0), axis=0, keepdims=True)
+    ours = group == lane // steps
+    spots = jnp.broadcast_to(spots, shape)
+    before = jnp.sum(jnp.where(ours & (spots < lane % steps), 1, 0), axis=0, keepdims=True)
+    table[1:2, :] = lane[0:1, :] % steps - before
+    table[2:3, :] = jnp.sum(jnp.where(ours & (spots == lane % steps), 1, 0), axis=0, keepdims=True)
 
 
 def place_kernel(fsdp, per_slice, owners_ref, returned_ref, update_ref, held, counts, in_sems, out_sems):
@@ -505,7 +545,7 @@
         counts[owner] = 0
     takes, puts = [], []
     for b in range(per_slice):
-        owner = owners_ref[base + b, 0]
+        owner = owners_ref[base + b]
         count = counts[owner]
         counts[owner] = count + 1
         takes.append(
@@ -528,7 +568,7 @@
     slots = sketch.shape[2]
     per_slice = block_total // rep
     steps = slots * fsdp
-    table_width = -(-rep * steps // 128) * 128
+    table_width = -(-max(rep * steps, block_total) // 128) * 128
     hbm = pl.BlockSpec(memory_space=pl.ANY)
     vmem = pl.BlockSpec(memory_space=pltpu.VMEM)
     smem = pl.BlockSpec(memory_space=pltpu.SMEM)
@@ -541,15 +581,18 @@
             jax.ShapeDtypeStruct((slots, fsdp) + block, BF),
             jax.ShapeDtypeStruct((slots, width, rank), BF),
         ),
-        in_specs=[vmem, vmem, hbm],
+        in_specs=[vmem, hbm, hbm],
         out_specs=(hbm, vmem),
         scratch_shapes=[
             pltpu.VMEM((per_slice,) + block, BF),
             pltpu.VMEM((per_slice,) + block, BF),
             pltpu.VMEM((per_slice,) + block, BF),
             pltpu.VMEM((per_slice,) + block, BF),
-            pltpu.VMEM((steps,) + block, BF),
-            pltpu.VMEM((steps,) + block, BF),
+            pltpu.VMEM((slots, width, rank), BF),
+            pltpu.VMEM((per_slice,) + block, BF),
+            pltpu.VMEM((2, per_slice) + block, BF),
+            pltpu.VMEM((per_slice,) + block, BF),
+            pltpu.VMEM((2 * steps - per_slice,) + block, BF),
             pltpu.VMEM((steps,) + block, BF),
             pltpu.VMEM((slots, fsdp) + block, BF),
             pltpu.VMEM((slots, fsdp) + block, BF),
@@ -561,11 +604,11 @@
             pltpu.VMEM((8, width), F32),
             pltpu.VMEM((rep, 8, 128), F32),
             pltpu.VMEM((fsdp, 8, 128), F32),
-            pltpu.VMEM((2, table_width), jnp.int32),
-            pltpu.SMEM((2, table_width), jnp.int32),
-            dma((2,)),
-            dma((2, 2)),
-            dma((2, steps)),
+            pltpu.VMEM((3, table_width), jnp.int32),
+            pltpu.SMEM((3, table_width), jnp.int32),
+            dma((rep + 1,)),
+            dma((2, 2, per_slice)),
+            dma((2, per_slice)),
             dma((2, steps)),
             dma((2, rep)),
             dma((2, fsdp)),
@@ -577,7 +620,7 @@
             collective_id=0, has_side_effects=True, vmem_limit_bytes=VMEM_BYTES
         ),
         name="step",
-    )(owner_table, sketch[0, 0], partials)
+    )(owner_table.reshape(1, block_total), sketch[0, 0], partials)
     updates = pl.pallas_call(
         functools.partial(place_kernel, fsdp, per_slice),
         out_shape=jax.ShapeDtypeStruct((per_slice,) + block, BF),
@@ -590,11 +633,11 @@
             dma((per_slice,)),
         ],
         name="place",
-    )(owner_table, returned)
+    )(owner_table.reshape(block_total), returned)
     return (updates, fresh[None, None])
 
 
-VMEM_BYTES = 60 * 1024 * 1024
+VMEM_BYTES = 62 * 1024 * 1024
 
 
 def choose(partials, sketch, owner_table):
@@ -603,9 +646,9 @@
     rep = lax.axis_size("rep")
     steps = sketch.shape[2] * fsdp
     per_slice = block_total // rep
-    pairs = rep == 4 and fsdp & (fsdp - 1) == 0
-    needed = (4 * per_slice + 5 * steps) * rows * width * 2
-    if pairs and needed < VMEM_BYTES - (12 << 20):
+    pairs = rep == 4 and fsdp & (fsdp - 1) == 0 and fsdp >= 4 and 2 * fsdp >= steps >= per_slice > steps - fsdp
+    needed = (7 * per_slice + 5 * steps) * rows * width * 2
+    if pairs and needed < VMEM_BYTES - (10 << 20):
         return fused(partials, sketch, owner_table)
     return local(partials, sketch, owner_table)
 

time: 233 us -> 217 us (0.931)
  Pallas kernels: 230 us -> 215 us
    pallas_call x1, Pallas kernels: 225 us -> 211 us  [fused(): pl.pallas_call(functools.partial(step_kernel, fsdp, slots, per_slice, cli...]
where the time goes in v1:
time: 217 us; the launch traced here: 216 us
  Pallas kernels  215 us (99%)
    pallas_call x1, Pallas kernels, fused(): pl.pallas_call(functools.partial(step_kernel, fsdp, slots, per_slice, cli...  211 us

profile of v1, /device:TPU:0, one launch (start us, length us, event | category | flops | bytes accessed | tf_op | source)
XLA Modules:
  0.0 216.5 jit_solution(11559236951786812255)
XLA Ops:
  0.6 210.8 %step.1 = (bf16[2,8,128,1024]{3,2,1,0:T(8,128)(2,1)}, bf16[2,1024,256]{2,1,0:T(8,128)(2,1)}) custom-call(s32[1,56]{1,0:T(1,128)} %bitcast.6, bf16[2,1024,256]{2,1,0:T(8,128)(2,1)} %bitcast.4, bf16[1,56,128,1024]{3,2,1,0:T(8,128)(2,1)} %partials_ref.1), custom_call_target="tpu_custom_call" | custom-call | tf_op jit(solution)/shard_map/step/pallas_call | solution.py:578
  211.4 0.0 copy-start
  211.4 4.1 %place.1 = bf16[14,128,1024]{2,1,0:T(8,128)(2,1)} custom-call(s32[56]{0:T(128)} %bitcast.7, bf16[2,8,128,1024]{3,2,1,0:T(8,128)(2,1)} %get-tuple-element.4.returned_ref), custom_call_target="tpu_custom_call" | custom-call | tf_op jit(solution)/shard_map/place/pallas_call | solution.py:624
  215.5 0.0 copy-done
  215.5 1.0 copy.6
Async XLA Ops:
  211.4 4.1 %copy-start = (bf16[2,1024,256]{2,1,0:T(8,128)(2,1)S(1)}, bf16[2,1024,256]{2,1,0:T(8,128)(2,1)}, u32[]{:S(2)}) copy-start(bf16[2,1024,256]{2,1,0:T(8,128)(2,1)} %get-tuple-element.5) | copy-start | bytes 3145732

commit v2 on v1

--- a/solution.py
+++ b/solution.py
@@ -207,9 +207,10 @@
 
 def step_kernel(
     fsdp, slots, per_slice, clip_limit, owners_ref, sketch_ref, partials_ref, returned_ref, fresh_ref,
-    held_0, held_1, held_2, held_3, sketch_held, staged, paired, crossed, totals, summed, incoming, updates, narrow_t, side_t, wide, basis, basis_low,
+    held_0, held_1, held_2, held_3, sketch_held, staged, paired, crossed, totals, summed, incoming, updates, landing, factor_in, basis_in, narrow_t, side_t, wide, basis, basis_low,
     square_acc, rep_squares, fsdp_squares, table, scalars,
     load_sems, pair_sems, cross_sems, owner_sems, rep_sems, fsdp_sems, home_sems, self_sems, table_sem,
+    basis_sends, basis_recvs, factor_sends, factor_recvs, land_sends, land_recvs, far_sems,
 ):
     bits = fsdp.bit_length() - 1
     half = fsdp // 2
@@ -406,17 +407,117 @@
     lax.fori_loop(0, per_slice, staged_out, 0)
     identity = eye_of(rank)
 
-    def home_copy(k, i):
-        home = flip(me_f, fsdp - 1 - i // 2 - half * (i % 2), bits)
+    side = me_f % 2
+    top = me_f // half
+    base = half * top
+    other = half - base
+    parts = width // tile
+    groups = half // 2
+    relay = half + side - 2 * top
+    is_relay = me_f // 2 == groups - 1 + top
+
+    def columns(p):
+        return pl.ds(pl.multiple_of(p * tile, tile), tile)
+
+    def basis_copy(k, group):
         return remote(
-            updates.at[k, i], returned_ref.at[k, me_f], home_sems.at[0, k, i], home_sems.at[1, k, i],
-            {"fsdp": home},
+            basis_low.at[k, pl.ds(pl.multiple_of(other * rows, rows), half * rows)],
+            basis_in.at[k, group],
+            basis_sends.at[k],
+            basis_recvs.at[k, group],
+            {"fsdp": relay},
+        )
+
+    def factor_copy(k, group, p):
+        return remote(
+            side_t.at[k, :, columns(p)],
+            factor_in.at[k, group, :, columns(p)],
+            factor_sends.at[k, p],
+            factor_recvs.at[k, group, p],
+            {"fsdp": relay},
+        )
+
+    def land_copy(k, group, e, p):
+        return remote(
+            incoming.at[k, group * half + e, :, columns(p)],
+            landing.at[k, 2 * group + side, :, columns(p)],
+            land_sends.at[k, group, e, p],
+            land_recvs.at[k, 2 * group + side, p],
+            {"fsdp": base + e},
+        )
+
+    def landed(k, q, p):
+        return remote(
+            incoming.at[k, q, :, columns(p)],
+            landing.at[k, q, :, columns(p)],
+            land_sends.at[k, 0, 0, p],
+            land_recvs.at[k, q, p],
+            {"fsdp": relay},
+        )
+
+    def home_copy(k, mask):
+        return remote(
+            updates.at[k, mask], returned_ref.at[k, me_f], home_sems.at[0, k, mask], home_sems.at[1, k, mask],
+            {"fsdp": flip(me_f, mask, bits)},
         )
 
     def self_copy(k):
+        return pltpu.make_async_copy(updates.at[k, 0], returned_ref.at[k, me_f], self_sems.at[k])
+
+    def far_place(m):
+        return 2 * (half - 1 - m)
+
+    def far_copy(k, m):
         return pltpu.make_async_copy(
-            updates.at[k, fsdp - 1], returned_ref.at[k, me_f], self_sems.at[k]
-        )
+            summed.at[k * fsdp + far_place(m)],
+            returned_ref.at[k, flip(me_f, half + m, bits)],
+            far_sems.at[k, m],
+        )
+
+    def pass_on(k):
+        def step(n, carry):
+            p = n // groups
+            group = n % groups
+
+            @pl.when(p == 0)
+            def _():
+                basis_copy(k, group).wait_recv()
+
+            factor_copy(k, group, p).wait_recv()
+            product = mm(basis_in[k, group], factor_in[k, group, :, columns(p)]).astype(BF)
+            for e in range(half):
+                piece = product[e * rows : (e + 1) * rows]
+
+                @pl.when(e == me_f - base)
+                def _():
+                    landing[k, 2 * group + side, :, columns(p)] = piece
+
+                @pl.when(e != me_f - base)
+                def _():
+                    incoming[k, group * half + e, :, columns(p)] = piece
+                    land_copy(k, group, e, p).start()
+
+            return carry
+
+        lax.fori_loop(0, parts * groups, step, 0)
+
+    def combine(k):
+        def one(m, carry):
+            q = flip(me_f, half + m, bits) - other
+            i = k * fsdp + far_place(m)
+            owner_copy(i).wait_send()
+
+            @pl.when((q % 2 != side) | (me_f // 2 != groups - 1 + top))
+            def _():
+                for p in range(parts):
+                    landed(k, q, p).wait_recv()
+
+            gradient = (clip_factor * summed[i].astype(F32)).astype(BF).astype(F32)
+            summed[i] = (gradient + landing[k, q].astype(F32)).astype(BF)
+            far_copy(k, m).start()
+            return carry
+
+        lax.fori_loop(0, half, one, 0)
 
     clip_factor = None
     for k in range(slots):
@@ -447,7 +548,8 @@
         full = mm3(powered_s, root)
         basis[...] = full
         low = full.astype(BF)
-        basis_low[...] = low
+        basis_low[k] = low
+        basis_copy(k, me_f % half // 2).start()
         project(k, low.T, clip_factor)
         coefficients_t = narrow_t[...]
         align_s = split(mm(sketch_t, low))
@@ -455,50 +557,83 @@
         energy = DECAY * mm3(align_t, align_s) + mm_last(coefficients_t, coefficients_t)
         root_inverse = kernel_root(energy + DAMPING * identity, 0.0, identity)
         mix = split(math.sqrt(DAMPING) * root_inverse - identity)
-        side_t[...] = (mm(mix[0], coefficients_t) + mm(mix[1], coefficients_t)).astype(BF)
+        for part in range(parts):
+            span = slice(part * tile, (part + 1) * tile)
+            chosen = coefficients_t[:, span]
+            side_t[k, :, span] = (mm(mix[0], chosen) + mm(mix[1], chosen)).astype(BF)
+            factor_copy(k, me_f % half // 2, part).start()
 
         def send(i, carry):
-            home = flip(me_f, fsdp - 1 - i // 2 - half * (i % 2), bits)
+            mask = half - 1 - i
+            home = flip(me_f, mask, bits)
             start = pl.multiple_of(home * rows, rows)
             gradient = (clip_factor * incoming[k, home].astype(F32)).astype(BF).astype(F32)
-            updates[k, i] = (
-                gradient + mm(basis_low[pl.ds(start, rows), :], side_t[...])
+            updates[k, mask] = (
+                gradient + mm(basis_low[k, pl.ds(start, rows), :], side_t[k])
             ).astype(BF)
 
-            @pl.when(i == fsdp - 1)
+            @pl.when(mask == 0)
             def _():
                 self_copy(k).start()
 
-            @pl.when(i != fsdp - 1)
+            @pl.when(mask != 0)
             def _():
-                home_copy(k, i).start()
+                home_copy(k, mask).start()
 
             return carry
 
-        lax.fori_loop(0, fsdp, send, 0)
+        lax.fori_loop(0, half, send, 0)
         inner_part = split(mm3(split(energy), split(root_inverse)))
         new_block = mm3(split(basis[...]), inner_part).astype(BF)
         active = scalars[2, me_r * steps + k * fsdp + fsdp - 1]
         fresh_ref[k] = jnp.where(active > 0, new_block, sketch)
 
-    def finish(i, carry):
-        slot, mask, owner = where(i)
-
-        @pl.when(mask != 0)
+    for k in range(slots):
+
+        @pl.when(is_relay)
         def _():
-            owner_copy(i).wait_send()
-
+            pass_on(k)
+
+        combine(k)
+
+    def finish(mask, carry):
+        for k in range(slots):
+            owner_copy(k * fsdp + 2 * (half - 1 - mask) + 1).wait_send()
+            home_copy(k, mask).wait()
         return carry
 
-    lax.fori_loop(0, steps, finish, 0)
-
-    def finish_home(i, carry):
+    lax.fori_loop(1, half, finish, 0)
+
+    def finish_parts(p, carry):
         for k in range(slots):
-            home_copy(k, i).wait()
+            factor_copy(k, 0, p).wait_send()
         return carry
 
-    lax.fori_loop(0, fsdp - 1, finish_home, 0)
+    lax.fori_loop(0, parts, finish_parts, 0)
+
+    @pl.when(is_relay)
+    def _():
+        def drain(n, carry):
+            group = n // (half * parts)
+            e = n // parts % half
+
+            @pl.when(e != me_f - base)
+            def _():
+                for k in range(slots):
+                    land_copy(k, group, e, n % parts).wait_send()
+
+            return carry
+
+        lax.fori_loop(0, groups * half * parts, drain, 0)
+
+    def finish_far(m, carry):
+        for k in range(slots):
+            far_copy(k, m).wait()
+        return carry
+
+    lax.fori_loop(0, half, finish_far, 0)
     for k in range(slots):
+        basis_copy(k, 0).wait_send()
         self_copy(k).wait()
 
 
@@ -574,6 +709,9 @@
     smem = pl.BlockSpec(memory_space=pltpu.SMEM)
     dma = pltpu.SemaphoreType.DMA
     block = (rows, width)
+    half = fsdp // 2
+    groups = half // 2
+    parts = width // rank
     clip_limit = 0.5 * math.sqrt(block_total * width * width)
     returned, fresh = pl.pallas_call(
         functools.partial(step_kernel, fsdp, slots, per_slice, clip_limit),
@@ -596,11 +734,14 @@
             pltpu.VMEM((steps,) + block, BF),
             pltpu.VMEM((slots, fsdp) + block, BF),
             pltpu.VMEM((slots, fsdp) + block, BF),
+            pltpu.VMEM((slots, half) + block, BF),
+            pltpu.VMEM((slots, groups, rank, width), BF),
+            pltpu.VMEM((slots, groups, half * rows, rank), BF),
             pltpu.VMEM((rank, width), BF),
-            pltpu.VMEM((rank, width), BF),
+            pltpu.VMEM((slots, rank, width), BF),
             pltpu.VMEM((width, rank), F32),
             pltpu.VMEM((width, rank), F32),
-            pltpu.VMEM((width, rank), BF),
+            pltpu.VMEM((slots, width, rank), BF),
             pltpu.VMEM((8, width), F32),
             pltpu.VMEM((rep, 8, 128), F32),
             pltpu.VMEM((fsdp, 8, 128), F32),
@@ -612,9 +753,16 @@
             dma((2, steps)),
             dma((2, rep)),
             dma((2, fsdp)),
-            dma((2, slots, fsdp)),
+            dma((2, slots, half)),
             dma((slots,)),
             dma,
+            dma((slots,)),
+            dma((slots, groups)),
+            dma((slots, parts)),
+            dma((slots, groups, parts)),
+            dma((slots, groups, half, parts)),
+            dma((slots, half, parts)),
+            dma((slots, half)),
         ],
         compiler_params=pltpu.CompilerParams(
             collective_id=0, has_side_effects=True, vmem_limit_bytes=VMEM_BYTES

time: 217 us -> 206 us (0.949)
  Pallas kernels: 215 us -> 204 us
    pallas_call x1, Pallas kernels: 211 us -> 200 us  [fused(): pl.pallas_call(functools.partial(step_kernel, fsdp, slots, per_slice, cli...]
where the time goes in v2:
time: 206 us
  Pallas kernels  204 us (99%)
    pallas_call x1, Pallas kernels, fused(): pl.pallas_call(functools.partial(step_kernel, fsdp, slots, per_slice, cli...  200 us

profile of v2, /device:TPU:0, one launch (start us, length us, event | category | flops | bytes accessed | tf_op | source)
XLA Modules:
  0.0 206.1 jit_solution(7490141428229865948)
XLA Ops:
  0.6 200.4 %step.1 = (bf16[2,8,128,1024]{3,2,1,0:T(8,128)(2,1)}, bf16[2,1024,256]{2,1,0:T(8,128)(2,1)}) custom-call(s32[1,56]{1,0:T(1,128)} %bitcast.6, bf16[2,1024,256]{2,1,0:T(8,128)(2,1)} %bitcast.4, bf16[1,56,128,1024]{3,2,1,0:T(8,128)(2,1)} %partials_ref.1), custom_call_target="tpu_custom_call" | custom-call | tf_op jit(solution)/shard_map/step/pallas_call | solution.py:716
  201.0 0.0 copy-start
  201.0 4.1 %place.1 = bf16[14,128,1024]{2,1,0:T(8,128)(2,1)} custom-call(s32[56]{0:T(128)} %bitcast.7, bf16[2,8,128,1024]{3,2,1,0:T(8,128)(2,1)} %get-tuple-element.4.returned_ref), custom_call_target="tpu_custom_call" | custom-call | tf_op jit(solution)/shard_map/place/pallas_call | solution.py:772
  205.1 0.0 copy-done
  205.1 1.0 copy.6
Async XLA Ops:
  201.0 4.1 %copy-start = (bf16[2,1024,256]{2,1,0:T(8,128)(2,1)S(1)}, bf16[2,1024,256]{2,1,0:T(8,128)(2,1)}, u32[]{:S(2)}) copy-start(bf16[2,1024,256]{2,1,0:T(8,128)(2,1)} %get-tuple-element.5) | copy-start | bytes 3145732

commit v3 on v2

--- a/solution.py
+++ b/solution.py
@@ -205,17 +205,39 @@
     return inverse / jnp.sqrt(trace_sum)
 
 
+def cell_order(fsdp, slots, per_slice):
+    half = fsdp // 2
+    near = range(half - 1, 0, -1)
+    cells = [(k, mask) for k in range(slots) for mask in range(fsdp - 1, half - 1, -1)]
+    cells += [(0, mask) for mask in near]
+    rest = [(k, mask) for k in range(1, slots) for mask in near]
+    kept = len(rest) - (slots * fsdp - per_slice)
+    return cells + rest[:kept] + [(k, 0) for k in range(slots)] + rest[kept:]
+
+
+def look_up(index, entries):
+    result = 0
+    for n, entry in enumerate(entries):
+        result = result + jnp.where(index == n, entry, 0)
+    return result
+
+
 def step_kernel(
     fsdp, slots, per_slice, clip_limit, owners_ref, sketch_ref, partials_ref, returned_ref, fresh_ref,
     held_0, held_1, held_2, held_3, sketch_held, staged, paired, crossed, totals, summed, incoming, updates, landing, factor_in, basis_in, narrow_t, side_t, wide, basis, basis_low,
-    square_acc, rep_squares, fsdp_squares, table, scalars,
+    square_acc, rep_squares, fsdp_squares, half_squares, table, scalars,
     load_sems, pair_sems, cross_sems, owner_sems, rep_sems, fsdp_sems, home_sems, self_sems, table_sem,
-    basis_sends, basis_recvs, factor_sends, factor_recvs, land_sends, land_recvs, far_sems,
+    basis_sends, basis_recvs, factor_sends, factor_recvs, land_sends, land_recvs, far_sems, half_sends, half_recv,
 ):
     bits = fsdp.bit_length() - 1
     half = fsdp // 2
     steps = slots * fsdp
     empty = steps - per_slice
+    cells = cell_order(fsdp, slots, per_slice)
+
+    def spot_of(k, mask):
+        return look_up(k * fsdp + mask, [cells.index((n // fsdp, n % fsdp)) for n in range(steps)])
+
     rows = incoming.shape[2]
     width = incoming.shape[3]
     rank = sketch_ref.shape[2]
@@ -275,9 +297,8 @@
         load.wait()
 
     def where(i):
-        place = i % fsdp
-        mask = fsdp - 1 - place // 2 - half * (place % 2)
-        return i // fsdp, mask, flip(me_f, mask, bits)
+        code = look_up(i, [k * fsdp + mask for k, mask in cells])
+        return code // fsdp, code % fsdp, flip(me_f, code % fsdp, bits)
 
     def cross_copy(k):
         return remote(
@@ -344,11 +365,11 @@
     lax.fori_loop(0, per_slice, both, 0)
 
     def arrived(k):
-        def wait_one(n, carry):
-            owner_copy(k * fsdp + n).wait_recv()
+        def wait_one(mask, carry):
+            owner_copy(spot_of(k, mask)).wait_recv()
             return carry
 
-        lax.fori_loop(0, fsdp - 1, wait_one, 0)
+        lax.fori_loop(1, fsdp, wait_one, 0)
 
     def wide_part(k, part):
         return incoming[k, :, :, part * tile : (part + 1) * tile].reshape(width, tile)
@@ -382,14 +403,14 @@
     for r in range(1, 4):
         lanes = lanes + rep_squares[r]
     fsdp_squares[me_f] = lanes
-    fsdp_copies = [
+    half_copies = [
         remote(
-            fsdp_squares.at[me_f], fsdp_squares.at[me_f], fsdp_sems.at[0, d], fsdp_sems.at[1, d],
-            {"fsdp": (me_f + d) % fsdp},
-        )
-        for d in range(1, fsdp)
+            fsdp_squares.at[me_f], fsdp_squares.at[me_f], fsdp_sems.at[0, mask], fsdp_sems.at[1, mask],
+            {"fsdp": flip(me_f, mask, bits)},
+        )
+        for mask in range(1, half)
     ]
-    for copy in fsdp_copies:
+    for copy in half_copies:
         copy.start()
 
     def last(i, carry):
@@ -405,14 +426,32 @@
         return carry
 
     lax.fori_loop(0, per_slice, staged_out, 0)
-    identity = eye_of(rank)
-
     side = me_f % 2
     top = me_f // half
     base = half * top
     other = half - base
     parts = width // tile
     groups = half // 2
+    at_end = me_f // 2 == top * (2 * groups - 1)
+    for copy in half_copies:
+        copy.wait()
+    lanes = fsdp_squares[base]
+    for e in range(1, half):
+        lanes = lanes + fsdp_squares[base + e]
+    half_squares[top] = lanes
+
+    def half_copy(source, e):
+        return remote(
+            half_squares.at[source], half_squares.at[source], half_sends.at[e], half_recv,
+            {"fsdp": other + 2 * e + side},
+        )
+
+    @pl.when(at_end)
+    def _():
+        for e in range(groups):
+            half_copy(top, e).start()
+
+    identity = eye_of(rank)
     relay = half + side - 2 * top
     is_relay = me_f // 2 == groups - 1 + top
 
@@ -464,25 +503,17 @@
     def self_copy(k):
         return pltpu.make_async_copy(updates.at[k, 0], returned_ref.at[k, me_f], self_sems.at[k])
 
-    def far_place(m):
-        return 2 * (half - 1 - m)
-
     def far_copy(k, m):
         return pltpu.make_async_copy(
-            summed.at[k * fsdp + far_place(m)],
+            summed.at[spot_of(k, half + m)],
             returned_ref.at[k, flip(me_f, half + m, bits)],
             far_sems.at[k, m],
         )
 
-    def pass_on(k):
-        def step(n, carry):
-            p = n // groups
-            group = n % groups
-
-            @pl.when(p == 0)
-            def _():
-                basis_copy(k, group).wait_recv()
-
+    def pass_on(k, turn, begin, end):
+        group = turn * top + (groups - 1 - turn) * (1 - top)
+
+        def step(p, carry):
             factor_copy(k, group, p).wait_recv()
             product = mm(basis_in[k, group], factor_in[k, group, :, columns(p)]).astype(BF)
             for e in range(half):
@@ -499,12 +530,16 @@
 
             return carry
 
-        lax.fori_loop(0, parts * groups, step, 0)
+        @pl.when(is_relay)
+        def _():
+            if begin == 0:
+                basis_copy(k, group).wait_recv()
+            lax.fori_loop(begin, end, step, 0)
 
     def combine(k):
         def one(m, carry):
             q = flip(me_f, half + m, bits) - other
-            i = k * fsdp + far_place(m)
+            i = spot_of(k, half + m)
             owner_copy(i).wait_send()
 
             @pl.when((q % 2 != side) | (me_f // 2 != groups - 1 + top))
@@ -533,11 +568,8 @@
             wide[span] = mm_last(incoming[k, part], projected_t)
             basis[span] = DECAY * mm(sketch[span], gram)
         if k == 0:
-            for copy in fsdp_copies:
-                copy.wait()
-            lanes = fsdp_squares[0]
-            for f in range(1, fsdp):
-                lanes = lanes + fsdp_squares[f]
+            half_copy(1 - top, 0).wait_recv()
+            lanes = half_squares[0] + half_squares[1]
             sum_squares = jnp.sum(lanes, keepdims=True)
             clip_factor = jnp.minimum(1.0, clip_limit / jnp.sqrt(sum_squares + 1e-06))
         powered_s = split(basis[...] + (clip_factor * clip_factor) * wide[...])
@@ -585,24 +617,37 @@
         lax.fori_loop(0, half, send, 0)
         inner_part = split(mm3(split(energy), split(root_inverse)))
         new_block = mm3(split(basis[...]), inner_part).astype(BF)
-        active = scalars[2, me_r * steps + k * fsdp + fsdp - 1]
+        active = scalars[2, me_r * steps + cells.index((k, 0))]
         fresh_ref[k] = jnp.where(active > 0, new_block, sketch)
 
-    for k in range(slots):
-
-        @pl.when(is_relay)
-        def _():
-            pass_on(k)
-
-        combine(k)
+    split_at = parts // 2
+    if slots == 2 and groups == 2:
+        pass_on(0, 0, 0, parts)
+        pass_on(1, 0, 0, parts)
+        pass_on(0, 1, 0, parts)
+        pass_on(1, 1, 0, split_at)
+        combine(0)
+        pass_on(1, 1, split_at, parts)
+        combine(1)
+    else:
+        for k in range(slots):
+            for turn in range(groups):
+                pass_on(k, turn, 0, parts)
+            combine(k)
 
     def finish(mask, carry):
         for k in range(slots):
-            owner_copy(k * fsdp + 2 * (half - 1 - mask) + 1).wait_send()
+            owner_copy(spot_of(k, mask)).wait_send()
             home_copy(k, mask).wait()
         return carry
 
     lax.fori_loop(1, half, finish, 0)
+
+    @pl.when(at_end)
+    def _():
+        for e in range(groups):
+            half_copy(top, e).wait_send()
+
 
     def finish_parts(p, carry):
         for k in range(slots):
@@ -640,7 +685,7 @@
 def fill_table(fsdp, slots, per_slice, me_f, owners_ref, table):
     total = owners_ref.shape[1]
     steps = slots * fsdp
-    half = fsdp // 2
+    cells = cell_order(fsdp, slots, per_slice)
     shape = (total, total)
     down = lax.broadcasted_iota(jnp.int32, shape, 0)
     along = lax.broadcasted_iota(jnp.int32, shape, 1)
@@ -655,8 +700,8 @@
     earlier = same & (owners == owners_along) & (along < down)
     ranks = jnp.sum(jnp.where(earlier, 1, 0), axis=1, keepdims=True)
     mask = lax.bitwise_xor(owners, jnp.full(shape, me_f, jnp.int32))
-    place = jnp.where(mask >= half, 2 * (fsdp - 1 - mask), 2 * (half - 1 - mask) + 1)
-    spot = jnp.broadcast_to(ranks, shape) * fsdp + place
+    cell = jnp.broadcast_to(ranks, shape) * fsdp + mask
+    spot = look_up(cell, [cells.index((n // fsdp, n % fsdp)) for n in range(steps)])
     ahead = jnp.sum(jnp.where(same & (turned(spot) < spot), 1, 0), axis=1, keepdims=True)
     spots = jnp.max(spot, axis=1, keepdims=True)
     shape = (total, table.shape[1])
@@ -745,6 +790,7 @@
             pltpu.VMEM((8, width), F32),
             pltpu.VMEM((rep, 8, 128), F32),
             pltpu.VMEM((fsdp, 8, 128), F32),
+            pltpu.VMEM((2, 8, 128), F32),
             pltpu.VMEM((3, table_width), jnp.int32),
             pltpu.SMEM((3, table_width), jnp.int32),
             dma((rep + 1,)),
@@ -763,6 +809,8 @@
             dma((slots, groups, half, parts)),
             dma((slots, half, parts)),
             dma((slots, half)),
+            dma((groups,)),
+            dma,
         ],
         compiler_params=pltpu.CompilerParams(
             collective_id=0, has_side_effects=True, vmem_limit_bytes=VMEM_BYTES
@@ -794,7 +842,7 @@
     rep = lax.axis_size("rep")
     steps = sketch.shape[2] * fsdp
     per_slice = block_total // rep
-    pairs = rep == 4 and fsdp & (fsdp - 1) == 0 and fsdp >= 4 and 2 * fsdp >= steps >= per_slice > steps - fsdp
+    pairs = rep == 4 and fsdp & (fsdp - 1) == 0 and fsdp >= 4 and steps >= per_slice >= steps - (fsdp // 2 - 1) * (sketch.shape[2] - 1)
     needed = (7 * per_slice + 5 * steps) * rows * width * 2
     if pairs and needed < VMEM_BYTES - (10 << 20):
         return fused(partials, sketch, owner_table)

time: 206 us -> 195 us (0.947)
  Pallas kernels: 204 us -> 193 us
    pallas_call x1, Pallas kernels: 200 us -> 189 us  [fused(): pl.pallas_call(functools.partial(step_kernel, fsdp, slots, per_slice, cli...]
where the time goes in v3:
time: 195 us
  Pallas kernels  193 us (99%)
    pallas_call x1, Pallas kernels, fused(): pl.pallas_call(functools.partial(step_kernel, fsdp, slots, per_slice, cli...  189 us
    pallas_call x1, Pallas kernels, fused(): pl.pallas_call(functools.partial(place_kernel, fsdp, per_slice), out_shap...  4.08 us

profile of v3, /device:TPU:0, one launch (start us, length us, event | category | flops | bytes accessed | tf_op | source)
XLA Modules:
  0.0 194.9 jit_solution(11023019071020995041)
XLA Ops:
  0.6 189.2 %step.1 = (bf16[2,8,128,1024]{3,2,1,0:T(8,128)(2,1)}, bf16[2,1024,256]{2,1,0:T(8,128)(2,1)}) custom-call(s32[1,56]{1,0:T(1,128)} %bitcast.6, bf16[2,1024,256]{2,1,0:T(8,128)(2,1)} %bitcast.4, bf16[1,56,128,1024]{3,2,1,0:T(8,128)(2,1)} %partials_ref.1), custom_call_target="tpu_custom_call" | custom-call | tf_op jit(solution)/shard_map/step/pallas_call | solution.py:761
  189.8 0.0 copy-start
  189.8 4.1 %place.1 = bf16[14,128,1024]{2,1,0:T(8,128)(2,1)} custom-call(s32[56]{0:T(128)} %bitcast.7, bf16[2,8,128,1024]{3,2,1,0:T(8,128)(2,1)} %get-tuple-element.4.returned_ref), custom_call_target="tpu_custom_call" | custom-call | tf_op jit(solution)/shard_map/place/pallas_call | solution.py:820
  193.9 0.0 copy-done
  193.9 1.0 copy.6
Async XLA Ops:
  189.8 4.1 %copy-start = (bf16[2,1024,256]{2,1,0:T(8,128)(2,1)S(1)}, bf16[2,1024,256]{2,1,0:T(8,128)(2,1)}, u32[]{:S(2)}) copy-start(bf16[2,1024,256]{2,1,0:T(8,128)(2,1)} %get-tuple-element.5) | copy-start | bytes 3145732

commit v4 on v3

--- a/solution.py
+++ b/solution.py
@@ -224,10 +224,10 @@
 
 def step_kernel(
     fsdp, slots, per_slice, clip_limit, owners_ref, sketch_ref, partials_ref, returned_ref, fresh_ref,
-    held_0, held_1, held_2, held_3, sketch_held, staged, paired, crossed, totals, summed, incoming, updates, landing, factor_in, basis_in, narrow_t, side_t, wide, basis, basis_low,
+    held_0, held_1, held_2, held_3, sketch_held, fresh_held, staged, paired, crossed, totals, summed, incoming, updates, landing, factor_in, basis_in, narrow_t, side_t, wide, basis, basis_low,
     square_acc, rep_squares, fsdp_squares, half_squares, table, scalars,
     load_sems, pair_sems, cross_sems, owner_sems, rep_sems, fsdp_sems, home_sems, self_sems, table_sem,
-    basis_sends, basis_recvs, factor_sends, factor_recvs, land_sends, land_recvs, far_sems, half_sends, half_recv,
+    basis_sends, basis_recvs, factor_sends, factor_recvs, land_sends, land_recvs, far_sems, half_sends, half_recv, fresh_sems,
 ):
     bits = fsdp.bit_length() - 1
     half = fsdp // 2
@@ -250,6 +250,7 @@
     across = (1 - row) * 2 + core
     partner_across = (1 - row) * 2 + 1 - core
     slices = (partner_across, partner, across, me_r)
+    early = (0, 2)
     held = (held_0, held_1, held_2, held_3)
     loads = [
         pltpu.make_async_copy(
@@ -258,8 +259,8 @@
         for n, number in enumerate(slices)
     ]
     loads.append(pltpu.make_async_copy(sketch_ref, sketch_held, load_sems.at[len(slices)]))
-    for load in loads:
-        load.start()
+    for n in early:
+        loads[n].start()
     fill_table(fsdp, slots, per_slice, me_f, owners_ref, table)
     publish = pltpu.make_async_copy(table, scalars, table_sem)
     publish.start()
@@ -267,10 +268,12 @@
         [{"rep": (me_r + d) % 4} for d in range(1, 4)]
         + [{"fsdp": (me_f + d) % fsdp} for d in range(1, fsdp)]
     )
+    for n, load in enumerate(loads):
+        if n not in early:
+            load.start()
     square_acc[...] = jnp.zeros_like(square_acc)
     publish.wait()
     loads[0].wait()
-    loads[1].wait()
 
     def block_at(n, k):
         return held[n][scalars[0, slices[n] * per_slice + k]]
@@ -283,18 +286,16 @@
             stage_ref(n, k), paired.at[n, k], pair_sems.at[0, n, k], pair_sems.at[1, n, k], {"rep": partner}
         )
 
-    def stage(k, carry):
-        for n in range(2):
+    def stage(n):
+        def step(k, carry):
             stage_ref(n, k)[...] = block_at(n, k)
             pair_copy(n, k).start()
-        return carry
-
-    lax.fori_loop(0, per_slice, stage, 0)
-    for n in range(empty):
-        totals[n] = jnp.zeros_like(totals[n])
-        totals[empty + per_slice + n] = jnp.zeros_like(totals[n])
-    for load in loads[2:]:
-        load.wait()
+            return carry
+
+        lax.fori_loop(0, per_slice, step, 0)
+
+    stage(0)
+    loads[2].wait()
 
     def where(i):
         code = look_up(i, [k * fsdp + mask for k, mask in cells])
@@ -352,6 +353,13 @@
         return carry
 
     lax.fori_loop(0, lag, first, 0)
+    loads[1].wait()
+    stage(1)
+    for n in range(empty):
+        totals[n] = jnp.zeros_like(totals[n])
+        totals[empty + per_slice + n] = jnp.zeros_like(totals[n])
+    for load in loads[3:]:
+        load.wait()
 
     def both(k, carry):
         @pl.when(k < per_slice - lag)
@@ -500,6 +508,9 @@
             {"fsdp": flip(me_f, mask, bits)},
         )
 
+    def fresh_copy(k):
+        return pltpu.make_async_copy(fresh_held.at[k], fresh_ref.at[k], fresh_sems.at[k])
+
     def self_copy(k):
         return pltpu.make_async_copy(updates.at[k, 0], returned_ref.at[k, me_f], self_sems.at[k])
 
@@ -555,6 +566,8 @@
         lax.fori_loop(0, half, one, 0)
 
     clip_factor = None
+    split_at = parts // 2
+    paired_turns = slots == 2 and groups == 2
     for k in range(slots):
         sketch = sketch_held[k]
         if k > 0:
@@ -583,6 +596,8 @@
         basis_low[k] = low
         basis_copy(k, me_f % half // 2).start()
         project(k, low.T, clip_factor)
+        if k == 1 and paired_turns:
+            pass_on(0, 0, 0, split_at)
         coefficients_t = narrow_t[...]
         align_s = split(mm(sketch_t, low))
         align_t = (align_s[0].T, align_s[1].T)
@@ -618,11 +633,11 @@
         inner_part = split(mm3(split(energy), split(root_inverse)))
         new_block = mm3(split(basis[...]), inner_part).astype(BF)
         active = scalars[2, me_r * steps + cells.index((k, 0))]
-        fresh_ref[k] = jnp.where(active > 0, new_block, sketch)
-
-    split_at = parts // 2
-    if slots == 2 and groups == 2:
-        pass_on(0, 0, 0, parts)
+        fresh_held[k] = jnp.where(active > 0, new_block, sketch)
+        fresh_copy(k).start()
+
+    if paired_turns:
+        pass_on(0, 0, split_at, parts)
         pass_on(1, 0, 0, parts)
         pass_on(0, 1, 0, parts)
         pass_on(1, 1, 0, split_at)
@@ -680,6 +695,7 @@
     for k in range(slots):
         basis_copy(k, 0).wait_send()
         self_copy(k).wait()
+        fresh_copy(k).wait()
 
 
 def fill_table(fsdp, slots, per_slice, me_f, owners_ref, table):
@@ -718,7 +734,10 @@
     table[2:3, :] = jnp.sum(jnp.where(ours & (spots == lane % steps), 1, 0), axis=0, keepdims=True)
 
 
-def place_kernel(fsdp, per_slice, owners_ref, returned_ref, update_ref, held, counts, in_sems, out_sems):
+def place_kernel(
+    fsdp, per_slice, owners_ref, returned_ref, fresh_ref, update_ref, kept_ref,
+    held, kept, counts, in_sems, out_sems, kept_sems,
+):
     base = lax.axis_index("rep") * per_slice
     last = returned_ref.shape[0] - 1
     for owner in range(fsdp):
@@ -732,10 +751,15 @@
             pltpu.make_async_copy(returned_ref.at[jnp.minimum(count, last), owner], held.at[b], in_sems.at[b])
         )
         takes[-1].start()
+    take_kept = pltpu.make_async_copy(fresh_ref, kept, kept_sems.at[0])
+    take_kept.start()
     for b in range(per_slice):
         takes[b].wait()
         puts.append(pltpu.make_async_copy(held.at[b], update_ref.at[b], out_sems.at[b]))
         puts[-1].start()
+    take_kept.wait()
+    puts.append(pltpu.make_async_copy(kept, kept_ref, kept_sems.at[1]))
+    puts[-1].start()
     for put in puts:
         put.wait()
 
@@ -765,12 +789,13 @@
             jax.ShapeDtypeStruct((slots, width, rank), BF),
         ),
         in_specs=[vmem, hbm, hbm],
-        out_specs=(hbm, vmem),
+        out_specs=(hbm, hbm),
         scratch_shapes=[
             pltpu.VMEM((per_slice,) + block, BF),
             pltpu.VMEM((per_slice,) + block, BF),
             pltpu.VMEM((per_slice,) + block, BF),
             pltpu.VMEM((per_slice,) + block, BF),
+            pltpu.VMEM((slots, width, rank), BF),
             pltpu.VMEM((slots, width, rank), BF),
             pltpu.VMEM((per_slice,) + block, BF),
             pltpu.VMEM((2, per_slice) + block, BF),
@@ -811,26 +836,32 @@
             dma((slots, half)),
             dma((groups,)),
             dma,
+            dma((slots,)),
         ],
         compiler_params=pltpu.CompilerParams(
             collective_id=0, has_side_effects=True, vmem_limit_bytes=VMEM_BYTES
         ),
         name="step",
     )(owner_table.reshape(1, block_total), sketch[0, 0], partials)
-    updates = pl.pallas_call(
+    updates, kept = pl.pallas_call(
         functools.partial(place_kernel, fsdp, per_slice),
-        out_shape=jax.ShapeDtypeStruct((per_slice,) + block, BF),
-        in_specs=[smem, hbm],
-        out_specs=hbm,
+        out_shape=(
+            jax.ShapeDtypeStruct((per_slice,) + block, BF),
+            jax.ShapeDtypeStruct((slots, width, rank), BF),
+        ),
+        in_specs=[smem, hbm, hbm],
+        out_specs=(hbm, hbm),
         scratch_shapes=[
             pltpu.VMEM((per_slice,) + block, BF),
+            pltpu.VMEM((slots, width, rank), BF),
             pltpu.SMEM((fsdp,), jnp.int32),
             dma((per_slice,)),
             dma((per_slice,)),
+            dma((2,)),
         ],
         name="place",
-    )(owner_table.reshape(block_total), returned)
-    return (updates, fresh[None, None])
+    )(owner_table.reshape(block_total), returned, fresh)
+    return (updates, kept[None, None])
 
 
 VMEM_BYTES = 62 * 1024 * 1024

time: 195 us -> 194 us (level)
  no operation moved by 1% of the time
where the time goes in v4:
time: 194 us
  Pallas kernels  193 us (99%)
    pallas_call x1, Pallas kernels, fused(): pl.pallas_call(functools.partial(step_kernel, fsdp, slots, per_slice, cli...  187 us
    pallas_call x1, Pallas kernels, fused(): pl.pallas_call(functools.partial(place_kernel, fsdp, per_slice), out_shap...  5.42 us

profile of v4, /device:TPU:0, one launch (start us, length us, event | category | flops | bytes accessed | tf_op | source)
XLA Modules:
  0.0 193.6 jit_solution(11466239686847179316)
XLA Ops:
  0.6 187.4 %step.1 = (bf16[2,8,128,1024]{3,2,1,0:T(8,128)(2,1)}, bf16[2,1024,256]{2,1,0:T(8,128)(2,1)}) custom-call(s32[1,56]{1,0:T(1,128)} %bitcast.5, bf16[2,1024,256]{2,1,0:T(8,128)(2,1)} %bitcast.4, bf16[1,56,128,1024]{3,2,1,0:T(8,128)(2,1)} %partials_ref.1), custom_call_target="tpu_custom_call" | custom-call | tf_op jit(solution)/shard_map/step/pallas_call | solution.py:785
  188.0 5.4 %place.1 = (bf16[14,128,1024]{2,1,0:T(8,128)(2,1)}, bf16[2,1024,256]{2,1,0:T(8,128)(2,1)}) custom-call(s32[56]{0:T(128)} %bitcast.6, bf16[2,8,128,1024]{3,2,1,0:T(8,128)(2,1)} %get-tuple-element.6.returned_ref, bf16[2,1024,256]{2,1,0:T(8,128)(2,1)} %get-tuple-element.7.fresh_ref), custom_call_target="tpu_custom_call" | custom-call | tf_op jit(solution)/shard_map/place/pallas_call | solution.py:846
